TPU v7x, 32 devices: a whole 2x2x4 slice. The times are simulated.
32 devices in a mesh: lat: 4 (over z), lon: 4 (over y, x), lev: 2 (over core).
Axes of the slice: x: 2, y: 2, z: 4, core: 2. Of those that a mesh axis runs over, the one named last changes fastest.
Arguments:
- initial_heat: float32 [64, 32, 192, 128], P('lat', 'lon', 'lev'), may hold values from 0.2 to 1.8
- scaled_wind_north: float32 [64, 32, 192, 128], P('lat', 'lon', 'lev'), may hold values from -0.3 to 0.3
- scaled_wind_east: float32 [64, 32, 192, 128], P('lat', 'lon', 'lev'), may hold values from -0.3 to 0.3
- scaled_wind_vertical: float32 [64, 32, 192, 128], P('lat', 'lon', 'lev'), may hold values from -0.3 to 0.3
Outputs:
- accumulated_eastward: float32 [64, 32, 192, 128], P('lat', 'lon', 'lev')
- temperature_end: float32 [64, 32, 192, 128], P('lat', 'lon', 'lev')
All inputs are finite; a program needn't handle non-finite values.
Results may differ from a plain program's by a relative error of at most 0.00002.
Values sent between devices are 32-bit elements; how exact they have to be, the bound alone decides.
A program may use at most 448 MiB of HBM per device.

v0:
```python
import jax
import jax.numpy as jnp
from jax import lax
from jax.sharding import PartitionSpec as P

STEPS = 6


def with_halo(cells, sides, width):
    for axis, dim in sides:
        count = lax.axis_size(axis)
        ends = count - 1
        head = lax.slice_in_dim(cells, 0, width, axis=dim)
        tail = lax.slice_in_dim(cells, cells.shape[dim] - width, cells.shape[dim], axis=dim)
        cells = jnp.concatenate(
            [
                lax.ppermute(tail, axis, [(i, (i + 1) % count) for i in range(ends)]),
                cells,
                lax.ppermute(head, axis, [((i + 1) % count, i) for i in range(ends)]),
            ],
            axis=dim,
        )
    return cells


def entering(part, axis, combine, identity):
    place = lax.axis_index(axis)
    gathered = lax.all_gather(part, axis)
    state = jnp.zeros_like(part) + jnp.asarray(identity, part.dtype)

    def one(hop, state):
        return combine(state, lax.dynamic_index_in_dim(gathered, hop, 0, False))

    return lax.fori_loop(0, place, one, state)


def strip_edges(values, dims):
    for dim in dims:
        values = lax.slice_in_dim(values, 1, values.shape[dim] - 1, axis=dim)
    return values


def neighbour(values, dim, start, dims):
    others = [other for other in dims if other != dim]
    values = strip_edges(values, others)
    return lax.slice_in_dim(values, start, start + values.shape[dim] - 2, axis=dim)


def single_update(extended_field, scaled_wind_north, scaled_wind_east, scaled_wind_vertical):
    middle = strip_edges(extended_field, (0, 1, 2))
    lower = [neighbour(extended_field, dim, 0, (0, 1, 2)) for dim in (0, 1, 2)]
    upper = [neighbour(extended_field, dim, 2, (0, 1, 2)) for dim in (0, 1, 2)]
    slopes = [above - beneath_layer for above, beneath_layer in zip(upper, lower)]
    smooth_rate = 0.05
    spread = lower[0] + upper[0] + lower[1] + upper[1] + lower[2] + upper[2] - 6.0 * middle
    return (
        middle
        - scaled_wind_north * slopes[0]
        - scaled_wind_east * slopes[1]
        - scaled_wind_vertical * slopes[2]
        + smooth_rate * spread
    )


def per_device(initial_heat, scaled_wind_north, scaled_wind_east, scaled_wind_vertical):
    for step in range(STEPS):
        extended_field = with_halo(initial_heat, (("lat", 0), ("lon", 1), ("lev", 2)), 1)
        initial_heat = single_update(
            extended_field, scaled_wind_north, scaled_wind_east, scaled_wind_vertical
        )
    present_layer = jnp.cumsum(initial_heat, axis=1)
    total = lax.slice_in_dim(
        present_layer, present_layer.shape[1] - 1, present_layer.shape[1], axis=1
    )

    def add_pair(earlier_total, later_total):
        return earlier_total + later_total

    beneath_layer = entering(total, "lon", add_pair, jnp.zeros_like(total))
    accumulated_eastward = (present_layer + beneath_layer) / (
        initial_heat.shape[1] * lax.axis_size("lon")
    )
    return (accumulated_eastward, initial_heat)


def solution(mesh):
    in_specs = (
        P("lat", "lon", "lev", None),
        P("lat", "lon", "lev", None),
        P("lat", "lon", "lev", None),
        P("lat", "lon", "lev", None),
    )
    out_specs = (P("lat", "lon", "lev", None), P("lat", "lon", "lev", None))
    return jax.shard_map(
        per_device, mesh=mesh, in_specs=in_specs, out_specs=out_specs, check_vma=False
    )
```

profile of v0, /device:TPU:22, one launch (start us, length us, event | category | flops | bytes accessed | tf_op | source)
XLA Modules:
  0.0 613.6 jit_solution(9463653932564070810)
XLA Ops:
  8.4 3.5 collective-permute-start.1
  11.9 2.4 collective-permute-start
  14.2 6.9 %collective-permute-done.1 = f32[1,8,96,128]{3,2,1,0:T(8,128)S(1)} collective-permute-done((f32[1,8,96,128]{3,2,1,0:T(8,128)S(1)}, f32[1,8,96,128]{3,2,1,0:T(8,128)S(1)}, u32[]{:S(2)}, u32[]{:S(2)}) %collective-permute-start.1) | collective-permute-done | bytes 393248 | tf_op jit(solution)/shard_map/ppermute | solution.py:17
  21.2 3.4 constant_dynamic-update-slice_fusion.1
  24.8 1.6 collective-permute-start.3
  26.4 5.0 collective-permute-start.2
  31.4 18.2 %collective-permute-done.3 = f32[18,1,96,128]{3,2,1,0:T(8,128)S(1)} collective-permute-done((f32[18,1,96,128]{3,2,1,0:T(8,128)S(1)}, f32[18,1,96,128]{3,2,1,0:T(8,128)S(1)}, u32[]{:S(2)}, u32[]{:S(2)}) %collective-permute-start.3) | collective-permute-done | bytes 884768 | tf_op jit(solution)/shard_map/ppermute | solution.py:17
  51.1 3.0 collective-permute-start.5
  55.2 25.6 %multiply_add_fusion.5 = f32[16,8,96,128]{3,2,1,0:T(8,128)} fusion(f32[16,8,96,128]{3,2,1,0:T(8,128)} %param.6, f32[16,8,96,128]{3,2,1,0:T(8,128)S(1)} %bitcast.10, f32[18,10,1,128]{3,2,1,0:T(1,128)S(1)} %copy.38, f32[18,1,96,128]{3,2,1,0:T(8,128)S(1)} %collective-permute-done.2, f32[18,8,96,128]{3,2,1,0:T(8,128)} %copy-done.5, ...), kind=kLoop, calls=%fused_computation.107 | loop fusion | flops 44040192 | bytes 41275392 | tf_op jit(solution)/shard_map/add | solution.py:57
  82.2 3.6 collective-permute-start.7
  85.8 2.4 collective-permute-start.6
  88.2 7.4 %collective-permute-done.7 = f32[1,8,96,128]{3,2,1,0:T(8,128)S(1)} collective-permute-done((f32[1,8,96,128]{3,2,1,0:T(8,128)S(1)}, f32[1,8,96,128]{3,2,1,0:T(8,128)S(1)}, u32[]{:S(2)}, u32[]{:S(2)}) %collective-permute-start.7) | collective-permute-done | bytes 393248 | tf_op jit(solution)/shard_map/ppermute | solution.py:17
  95.6 3.2 collective-permute-done.6
  98.8 1.5 pad_maximum_fusion.112
  101.6 19.1 %collective-permute-start.8 = (f32[18,1,96,128]{3,2,1,0:T(8,128)S(1)}, f32[18,1,96,128]{3,2,1,0:T(8,128)S(1)}, u32[]{:S(2)}, u32[]{:S(2)}) collective-permute-start(f32[18,1,96,128]{3,2,1,0:T(8,128)S(1)} %get-tuple-element.69), channel_id=1, source_target_pairs={{2,0},{4,2},{6,4},{3,1},{5,3},{7,5},{10,8},{12,10},{14,12},{11,9},... | collective-permute-start | bytes 2654216 | tf_op jit(solution)/shard_map/ppermute | solution.py:19
  120.7 18.5 %collective-permute-done.9 = f32[18,1,96,128]{3,2,1,0:T(8,128)S(1)} collective-permute-done((f32[18,1,96,128]{3,2,1,0:T(8,128)S(1)}, f32[18,1,96,128]{3,2,1,0:T(8,128)S(1)}, u32[]{:S(2)}, u32[]{:S(2)}) %collective-permute-start.9) | collective-permute-done | bytes 884768 | tf_op jit(solution)/shard_map/ppermute | solution.py:17
  141.5 3.0 collective-permute-start.11
  145.6 25.0 %multiply_add_fusion.4 = f32[16,8,96,128]{3,2,1,0:T(8,128)} fusion(f32[16,8,96,128]{3,2,1,0:T(8,128)} %multiply_add_fusion.5, f32[16,8,96,128]{3,2,1,0:T(8,128)S(1)} %bitcast.10, f32[18,10,1,128]{3,2,1,0:T(1,128)S(1)} %copy.42, f32[18,1,96,128]{3,2,1,0:T(8,128)} %copy-done.7, f32[1,8,96,128]{3,2,1,0:T(8,128)S(1)} %collective-permute-done.6, ...), kind=kLoop, calls=%fused_computation.106 | loop fusion | flops 56623104 | bytes 34197504 | tf_op jit(solution)/shard_map/add | solution.py:57
  170.7 1.3 fusion.4
  172.0 2.1 collective-permute-start.13
  174.1 3.9 collective-permute-start.12
  178.0 7.4 %collective-permute-done.13 = f32[1,8,96,128]{3,2,1,0:T(8,128)S(1)} collective-permute-done((f32[1,8,96,128]{3,2,1,0:T(8,128)S(1)}, f32[1,8,96,128]{3,2,1,0:T(8,128)S(1)}, u32[]{:S(2)}, u32[]{:S(2)}) %collective-permute-start.13) | collective-permute-done | bytes 393248 | tf_op jit(solution)/shard_map/ppermute | solution.py:17
  185.4 1.9 collective-permute-done.12
  187.4 1.5 pad_maximum_fusion.109
  190.2 19.6 %collective-permute-start.14 = (f32[18,1,96,128]{3,2,1,0:T(8,128)S(1)}, f32[18,1,96,128]{3,2,1,0:T(8,128)S(1)}, u32[]{:S(2)}, u32[]{:S(2)}) collective-permute-start(f32[18,1,96,128]{3,2,1,0:T(8,128)S(1)} %get-tuple-element.67), channel_id=1, source_target_pairs={{2,0},{4,2},{6,4},{3,1},{5,3},{7,5},{10,8},{12,10},{14,12},{11,9},... | collective-permute-start | bytes 2654216 | tf_op jit(solution)/shard_map/ppermute | solution.py:19
  209.8 18.5 %collective-permute-done.15 = f32[18,1,96,128]{3,2,1,0:T(8,128)S(1)} collective-permute-done((f32[18,1,96,128]{3,2,1,0:T(8,128)S(1)}, f32[18,1,96,128]{3,2,1,0:T(8,128)S(1)}, u32[]{:S(2)}, u32[]{:S(2)}) %collective-permute-start.15) | collective-permute-done | bytes 884768 | tf_op jit(solution)/shard_map/ppermute | solution.py:17
  230.6 3.2 collective-permute-start.17
  234.7 24.7 %multiply_add_fusion.3 = f32[16,8,96,128]{3,2,1,0:T(8,128)} fusion(f32[16,8,96,128]{3,2,1,0:T(8,128)} %multiply_add_fusion.4, f32[16,8,96,128]{3,2,1,0:T(8,128)S(1)} %bitcast.10, f32[18,10,1,128]{3,2,1,0:T(1,128)S(1)} %copy.46, f32[18,1,96,128]{3,2,1,0:T(8,128)} %copy-done.8, f32[1,8,96,128]{3,2,1,0:T(8,128)S(1)} %collective-permute-done.12, ...), kind=kLoop, calls=%fused_computation.105 | loop fusion | flops 56623104 | bytes 34197504 | tf_op jit(solution)/shard_map/add | solution.py:57
  260.7 2.1 collective-permute-start.19
  262.8 3.9 collective-permute-start.18
  266.7 7.4 %collective-permute-done.19 = f32[1,8,96,128]{3,2,1,0:T(8,128)S(1)} collective-permute-done((f32[1,8,96,128]{3,2,1,0:T(8,128)S(1)}, f32[1,8,96,128]{3,2,1,0:T(8,128)S(1)}, u32[]{:S(2)}, u32[]{:S(2)}) %collective-permute-start.19) | collective-permute-done | bytes 393248 | tf_op jit(solution)/shard_map/ppermute | solution.py:17
  274.1 1.9 collective-permute-done.18
  276.1 1.5 pad_maximum_fusion.106
  278.9 19.9 %collective-permute-start.20 = (f32[18,1,96,128]{3,2,1,0:T(8,128)S(1)}, f32[18,1,96,128]{3,2,1,0:T(8,128)S(1)}, u32[]{:S(2)}, u32[]{:S(2)}) collective-permute-start(f32[18,1,96,128]{3,2,1,0:T(8,128)S(1)} %get-tuple-element.65), channel_id=1, source_target_pairs={{2,0},{4,2},{6,4},{3,1},{5,3},{7,5},{10,8},{12,10},{14,12},{11,9},... | collective-permute-start | bytes 2654216 | tf_op jit(solution)/shard_map/ppermute | solution.py:19
  298.8 18.5 %collective-permute-done.21 = f32[18,1,96,128]{3,2,1,0:T(8,128)S(1)} collective-permute-done((f32[18,1,96,128]{3,2,1,0:T(8,128)S(1)}, f32[18,1,96,128]{3,2,1,0:T(8,128)S(1)}, u32[]{:S(2)}, u32[]{:S(2)}) %collective-permute-start.21) | collective-permute-done | bytes 884768 | tf_op jit(solution)/shard_map/ppermute | solution.py:17
  319.6 3.0 collective-permute-start.23
  323.7 25.0 %multiply_add_fusion.2 = f32[16,8,96,128]{3,2,1,0:T(8,128)} fusion(f32[16,8,96,128]{3,2,1,0:T(8,128)} %multiply_add_fusion.3, f32[16,8,96,128]{3,2,1,0:T(8,128)S(1)} %bitcast.10, f32[18,10,1,128]{3,2,1,0:T(1,128)S(1)} %copy.50, f32[18,1,96,128]{3,2,1,0:T(8,128)} %copy-done.9, f32[1,8,96,128]{3,2,1,0:T(8,128)S(1)} %collective-permute-done.18, ...), kind=kLoop, calls=%fused_computation.104 | loop fusion | flops 56623104 | bytes 34197504 | tf_op jit(solution)/shard_map/add | solution.py:57
  350.1 2.1 collective-permute-start.25
  352.1 3.9 collective-permute-start.24
  356.1 7.4 %collective-permute-done.25 = f32[1,8,96,128]{3,2,1,0:T(8,128)S(1)} collective-permute-done((f32[1,8,96,128]{3,2,1,0:T(8,128)S(1)}, f32[1,8,96,128]{3,2,1,0:T(8,128)S(1)}, u32[]{:S(2)}, u32[]{:S(2)}) %collective-permute-start.25) | collective-permute-done | bytes 393248 | tf_op jit(solution)/shard_map/ppermute | solution.py:17
  363.5 1.9 collective-permute-done.24
  365.4 1.5 pad_maximum_fusion.103
  368.2 19.9 %collective-permute-start.26 = (f32[18,1,96,128]{3,2,1,0:T(8,128)S(1)}, f32[18,1,96,128]{3,2,1,0:T(8,128)S(1)}, u32[]{:S(2)}, u32[]{:S(2)}) collective-permute-start(f32[18,1,96,128]{3,2,1,0:T(8,128)S(1)} %get-tuple-element.63), channel_id=1, source_target_pairs={{2,0},{4,2},{6,4},{3,1},{5,3},{7,5},{10,8},{12,10},{14,12},{11,9},... | collective-permute-start | bytes 2654216 | tf_op jit(solution)/shard_map/ppermute | solution.py:19
  388.1 18.5 %collective-permute-done.27 = f32[18,1,96,128]{3,2,1,0:T(8,128)S(1)} collective-permute-done((f32[18,1,96,128]{3,2,1,0:T(8,128)S(1)}, f32[18,1,96,128]{3,2,1,0:T(8,128)S(1)}, u32[]{:S(2)}, u32[]{:S(2)}) %collective-permute-start.27) | collective-permute-done | bytes 884768 | tf_op jit(solution)/shard_map/ppermute | solution.py:17
  408.9 3.3 collective-permute-start.29
  413.0 24.7 %multiply_add_fusion.1 = f32[16,8,96,128]{3,2,1,0:T(8,128)} fusion(f32[16,8,96,128]{3,2,1,0:T(8,128)} %multiply_add_fusion.2, f32[16,8,96,128]{3,2,1,0:T(8,128)S(1)} %bitcast.10, f32[18,10,1,128]{3,2,1,0:T(1,128)S(1)} %copy.54, f32[18,1,96,128]{3,2,1,0:T(8,128)} %copy-done.10, f32[1,8,96,128]{3,2,1,0:T(8,128)S(1)} %collective-permute-done.24, ...), kind=kLoop, calls=%fused_computation.103 | loop fusion | flops 56623104 | bytes 34197504 | tf_op jit(solution)/shard_map/add | solution.py:57
  437.7 1.3 fusion.1
  439.1 2.1 collective-permute-start.31
  441.1 3.9 collective-permute-start.30
  445.1 7.4 %collective-permute-done.31 = f32[1,8,96,128]{3,2,1,0:T(8,128)S(1)} collective-permute-done((f32[1,8,96,128]{3,2,1,0:T(8,128)S(1)}, f32[1,8,96,128]{3,2,1,0:T(8,128)S(1)}, u32[]{:S(2)}, u32[]{:S(2)}) %collective-permute-start.31) | collective-permute-done | bytes 393248 | tf_op jit(solution)/shard_map/ppermute | solution.py:17
  452.5 1.9 collective-permute-done.30
  454.4 1.5 pad_maximum_fusion.100
  457.2 19.9 %collective-permute-start.32 = (f32[18,1,96,128]{3,2,1,0:T(8,128)S(1)}, f32[18,1,96,128]{3,2,1,0:T(8,128)S(1)}, u32[]{:S(2)}, u32[]{:S(2)}) collective-permute-start(f32[18,1,96,128]{3,2,1,0:T(8,128)S(1)} %get-tuple-element.61), channel_id=1, source_target_pairs={{2,0},{4,2},{6,4},{3,1},{5,3},{7,5},{10,8},{12,10},{14,12},{11,9},... | collective-permute-start | bytes 2654216 | tf_op jit(solution)/shard_map/ppermute | solution.py:19
  477.1 18.5 %collective-permute-done.33 = f32[18,1,96,128]{3,2,1,0:T(8,128)S(1)} collective-permute-done((f32[18,1,96,128]{3,2,1,0:T(8,128)S(1)}, f32[18,1,96,128]{3,2,1,0:T(8,128)S(1)}, u32[]{:S(2)}, u32[]{:S(2)}) %collective-permute-start.33) | collective-permute-done | bytes 884768 | tf_op jit(solution)/shard_map/ppermute | solution.py:17
  497.9 3.0 collective-permute-start.35
  502.0 25.0 %multiply_add_fusion = f32[16,8,96,128]{3,2,1,0:T(8,128)} fusion(f32[16,8,96,128]{3,2,1,0:T(8,128)} %multiply_add_fusion.1, f32[16,8,96,128]{3,2,1,0:T(8,128)S(1)} %bitcast.10, f32[18,10,1,128]{3,2,1,0:T(1,128)S(1)} %copy.58, f32[18,1,96,128]{3,2,1,0:T(8,128)} %copy-done.11, f32[1,8,96,128]{3,2,1,0:T(8,128)S(1)} %collective-permute-done.30, ...), kind=kLoop, calls=%fused_computation.102 | loop fusion | flops 56623104 | bytes 34197504 | tf_op jit(solution)/shard_map/add | solution.py:57
  527.1 3.7 fusion.7
  530.8 2.7 copy-done.6
  534.4 61.9 %all-gather.3.cloned.1.call-done = f32[64,1,96,128]{3,2,1,0:T(8,128)} async-done(((f32[16,1,96,128]{3,2,1,0:T(8,128)}), f32[64,1,96,128]{3,2,1,0:T(8,128)}) %all-gather.3.cloned.1.call-update) | async-done | bytes 3145744 | tf_op jit(solution)/shard_map/all_gather | solution.py:28
  596.4 4.1 while.10
  596.4 1.3 bitcast_add_fusion.2
  597.7 1.3 bitcast_add_fusion.2
  599.1 1.3 bitcast_add_fusion.2
  600.4 6.3 %add_multiply_fusion = f32[16,8,96,128]{3,2,1,0:T(8,128)} fusion(f32[16,8,96,128]{3,2,1,0:T(8,128)} %copy-done.6, f32[16,96,128]{2,1,0:T(8,128)S(1)} %bitcast.13), kind=kLoop, calls=%fused_computation.101 | loop fusion | flops 3145728 | bytes 13369344 | tf_op jit(solution)/shard_map/div | solution.py:80
  (104 shorter events, 31.5 us)
Async XLA Ops:
  7.2 589.1 %all-gather.3.cloned.1.call-start = ((), (), s32[]{:S(2)}) async-start(), calls=%async_computation | async-start | bytes 3932160 | tf_op jit(solution)/shard_map/all_gather | solution.py:28
  8.4 12.7 %collective-permute-start.1 = (f32[1,8,96,128]{3,2,1,0:T(8,128)S(1)}, f32[1,8,96,128]{3,2,1,0:T(8,128)S(1)}, u32[]{:S(2)}, u32[]{:S(2)}) collective-permute-start(f32[1,8,96,128]{3,2,1,0:T(8,128)S(1)} %get-tuple-element.83), channel_id=1, source_target_pairs={{0,8},{8,16},{16,24},{1,9},{9,17},{17,25},{2,10},{10,18},{18,26},{... | collective-permute-start | bytes 1179656 | tf_op jit(solution)/shard_map/ppermute | solution.py:17
  11.9 12.7 %collective-permute-start = (f32[1,8,96,128]{3,2,1,0:T(8,128)S(1)}, f32[1,8,96,128]{3,2,1,0:T(8,128)S(1)}, u32[]{:S(2)}, u32[]{:S(2)}) collective-permute-start(f32[1,8,96,128]{3,2,1,0:T(8,128)S(1)} %get-tuple-element.82), channel_id=1, source_target_pairs={{8,0},{16,8},{24,16},{9,1},{17,9},{25,17},{10,2},{18,10},{26,18},{... | collective-permute-start | bytes 1179656 | tf_op jit(solution)/shard_map/ppermute | solution.py:19
  21.1 34.0 %slice-start.2 = ((s8[6291456]{0:T(1024)(128)(4,1)}), s8[4194304]{0:T(1024)(128)(4,1)S(1)}, s32[]{:S(2)}) async-start(s8[6291456]{0:T(1024)(128)(4,1)} %bitcast.11), calls=%async_computation.3 | async-start | bytes 8388608
  24.6 30.6 %slice-start.3 = ((s8[6291456]{0:T(1024)(128)(4,1)}), s8[2097152]{0:T(1024)(128)(4,1)S(1)}, s32[]{:S(2)}) async-start(s8[6291456]{0:T(1024)(128)(4,1)} %bitcast.11), calls=%async_computation.4 | async-start | bytes 4194304
  24.6 25.1 %copy-start.5 = (f32[18,8,96,128]{3,2,1,0:T(8,128)}, f32[18,8,96,128]{3,2,1,0:T(8,128)S(1)}, u32[]{:S(2)}) copy-start(f32[18,8,96,128]{3,2,1,0:T(8,128)S(1)} %constant_dynamic-update-slice_fusion) | copy-start | bytes 21233668
  24.6 30.6 %slice-start = ((s8[6291456]{0:T(1024)(128)(4,1)}), s8[4194304]{0:T(1024)(128)(4,1)S(1)}, s32[]{:S(2)}) async-start(s8[6291456]{0:T(1024)(128)(4,1)} %bitcast.9), calls=%async_computation.1 | async-start | bytes 8388608
  24.8 24.8 %collective-permute-start.3 = (f32[18,1,96,128]{3,2,1,0:T(8,128)S(1)}, f32[18,1,96,128]{3,2,1,0:T(8,128)S(1)}, u32[]{:S(2)}, u32[]{:S(2)}) collective-permute-start(f32[18,1,96,128]{3,2,1,0:T(8,128)S(1)} %get-tuple-element.70), channel_id=1, source_target_pairs={{0,2},{2,4},{4,6},{1,3},{3,5},{5,7},{8,10},{10,12},{12,14},{9,11},... | collective-permute-start | bytes 2654216 | tf_op jit(solution)/shard_map/ppermute | solution.py:17
  26.3 28.9 %slice-start.1 = ((s8[6291456]{0:T(1024)(128)(4,1)}), s8[2097152]{0:T(1024)(128)(4,1)S(1)}, s32[]{:S(2)}) async-start(s8[6291456]{0:T(1024)(128)(4,1)} %bitcast.9), calls=%async_computation.2 | async-start | bytes 4194304
  26.4 23.2 %collective-permute-start.2 = (f32[18,1,96,128]{3,2,1,0:T(8,128)S(1)}, f32[18,1,96,128]{3,2,1,0:T(8,128)S(1)}, u32[]{:S(2)}, u32[]{:S(2)}) collective-permute-start(f32[18,1,96,128]{3,2,1,0:T(8,128)S(1)} %get-tuple-element.71), channel_id=1, source_target_pairs={{2,0},{4,2},{6,4},{3,1},{5,3},{7,5},{10,8},{12,10},{14,12},{11,9},... | collective-permute-start | bytes 2654216 | tf_op jit(solution)/shard_map/ppermute | solution.py:19
  49.8 4.4 collective-permute-start.4
  51.1 4.0 collective-permute-start.5
  80.9 58.4 %copy-start.4 = (f32[16,8,96,128]{3,2,1,0:T(8,128)S(1)}, f32[16,8,96,128]{3,2,1,0:T(8,128)}, u32[]{:S(2)}) copy-start(f32[16,8,96,128]{3,2,1,0:T(8,128)} %multiply_add_fusion.5) | copy-start | bytes 18874372
  82.2 13.4 %collective-permute-start.7 = (f32[1,8,96,128]{3,2,1,0:T(8,128)S(1)}, f32[1,8,96,128]{3,2,1,0:T(8,128)S(1)}, u32[]{:S(2)}, u32[]{:S(2)}) collective-permute-start(f32[1,8,96,128]{3,2,1,0:T(8,128)S(1)} %get-tuple-element.80), channel_id=1, source_target_pairs={{0,8},{8,16},{16,24},{1,9},{9,17},{17,25},{2,10},{10,18},{18,26},{... | collective-permute-start | bytes 1179656 | tf_op jit(solution)/shard_map/ppermute | solution.py:17
  85.8 13.0 %collective-permute-start.6 = (f32[1,8,96,128]{3,2,1,0:T(8,128)S(1)}, f32[1,8,96,128]{3,2,1,0:T(8,128)S(1)}, u32[]{:S(2)}, u32[]{:S(2)}) collective-permute-start(f32[1,8,96,128]{3,2,1,0:T(8,128)S(1)} %get-tuple-element.81), channel_id=1, source_target_pairs={{8,0},{16,8},{24,16},{9,1},{17,9},{25,17},{10,2},{18,10},{26,18},{... | collective-permute-start | bytes 1179656 | tf_op jit(solution)/shard_map/ppermute | solution.py:19
  100.3 38.9 %collective-permute-start.9 = (f32[18,1,96,128]{3,2,1,0:T(8,128)S(1)}, f32[18,1,96,128]{3,2,1,0:T(8,128)S(1)}, u32[]{:S(2)}, u32[]{:S(2)}) collective-permute-start(f32[18,1,96,128]{3,2,1,0:T(8,128)S(1)} %get-tuple-element.68), channel_id=1, source_target_pairs={{0,2},{2,4},{4,6},{1,3},{3,5},{5,7},{8,10},{10,12},{12,14},{9,11},... | collective-permute-start | bytes 2654216 | tf_op jit(solution)/shard_map/ppermute | solution.py:17
  101.6 37.6 %collective-permute-start.8 = (f32[18,1,96,128]{3,2,1,0:T(8,128)S(1)}, f32[18,1,96,128]{3,2,1,0:T(8,128)S(1)}, u32[]{:S(2)}, u32[]{:S(2)}) collective-permute-start(f32[18,1,96,128]{3,2,1,0:T(8,128)S(1)} %get-tuple-element.69), channel_id=1, source_target_pairs={{2,0},{4,2},{6,4},{3,1},{5,3},{7,5},{10,8},{12,10},{14,12},{11,9},... | collective-permute-start | bytes 2654216 | tf_op jit(solution)/shard_map/ppermute | solution.py:19
  139.2 1.0 copy-start.7
  140.2 4.4 collective-permute-start.10
  141.5 4.0 collective-permute-start.11
  170.7 57.6 %copy-start = (f32[16,8,96,128]{3,2,1,0:T(8,128)S(1)}, f32[16,8,96,128]{3,2,1,0:T(8,128)}, u32[]{:S(2)}) copy-start(f32[16,8,96,128]{3,2,1,0:T(8,128)} %multiply_add_fusion.4) | copy-start | bytes 18874372
  172.0 13.4 %collective-permute-start.13 = (f32[1,8,96,128]{3,2,1,0:T(8,128)S(1)}, f32[1,8,96,128]{3,2,1,0:T(8,128)S(1)}, u32[]{:S(2)}, u32[]{:S(2)}) collective-permute-start(f32[1,8,96,128]{3,2,1,0:T(8,128)S(1)} %get-tuple-element.78), channel_id=1, source_target_pairs={{0,8},{8,16},{16,24},{1,9},{9,17},{17,25},{2,10},{10,18},{18,26},{... | collective-permute-start | bytes 1179656 | tf_op jit(solution)/shard_map/ppermute | solution.py:17
  174.1 13.3 %collective-permute-start.12 = (f32[1,8,96,128]{3,2,1,0:T(8,128)S(1)}, f32[1,8,96,128]{3,2,1,0:T(8,128)S(1)}, u32[]{:S(2)}, u32[]{:S(2)}) collective-permute-start(f32[1,8,96,128]{3,2,1,0:T(8,128)S(1)} %get-tuple-element.79), channel_id=1, source_target_pairs={{8,0},{16,8},{24,16},{9,1},{17,9},{25,17},{10,2},{18,10},{26,18},{... | collective-permute-start | bytes 1179656 | tf_op jit(solution)/shard_map/ppermute | solution.py:19
  188.9 39.4 %collective-permute-start.15 = (f32[18,1,96,128]{3,2,1,0:T(8,128)S(1)}, f32[18,1,96,128]{3,2,1,0:T(8,128)S(1)}, u32[]{:S(2)}, u32[]{:S(2)}) collective-permute-start(f32[18,1,96,128]{3,2,1,0:T(8,128)S(1)} %get-tuple-element.66), channel_id=1, source_target_pairs={{0,2},{2,4},{4,6},{1,3},{3,5},{5,7},{8,10},{10,12},{12,14},{9,11},... | collective-permute-start | bytes 2654216 | tf_op jit(solution)/shard_map/ppermute | solution.py:17
  190.2 38.1 %collective-permute-start.14 = (f32[18,1,96,128]{3,2,1,0:T(8,128)S(1)}, f32[18,1,96,128]{3,2,1,0:T(8,128)S(1)}, u32[]{:S(2)}, u32[]{:S(2)}) collective-permute-start(f32[18,1,96,128]{3,2,1,0:T(8,128)S(1)} %get-tuple-element.67), channel_id=1, source_target_pairs={{2,0},{4,2},{6,4},{3,1},{5,3},{7,5},{10,8},{12,10},{14,12},{11,9},... | collective-permute-start | bytes 2654216 | tf_op jit(solution)/shard_map/ppermute | solution.py:19
  228.3 1.0 copy-start.8
  229.3 4.6 collective-permute-start.16
  230.6 4.0 collective-permute-start.17
  259.4 57.9 %copy-start.1 = (f32[16,8,96,128]{3,2,1,0:T(8,128)S(1)}, f32[16,8,96,128]{3,2,1,0:T(8,128)}, u32[]{:S(2)}) copy-start(f32[16,8,96,128]{3,2,1,0:T(8,128)} %multiply_add_fusion.3) | copy-start | bytes 18874372
  260.7 13.4 %collective-permute-start.19 = (f32[1,8,96,128]{3,2,1,0:T(8,128)S(1)}, f32[1,8,96,128]{3,2,1,0:T(8,128)S(1)}, u32[]{:S(2)}, u32[]{:S(2)}) collective-permute-start(f32[1,8,96,128]{3,2,1,0:T(8,128)S(1)} %get-tuple-element.76), channel_id=1, source_target_pairs={{0,8},{8,16},{16,24},{1,9},{9,17},{17,25},{2,10},{10,18},{18,26},{... | collective-permute-start | bytes 1179656 | tf_op jit(solution)/shard_map/ppermute | solution.py:17
  262.8 13.3 %collective-permute-start.18 = (f32[1,8,96,128]{3,2,1,0:T(8,128)S(1)}, f32[1,8,96,128]{3,2,1,0:T(8,128)S(1)}, u32[]{:S(2)}, u32[]{:S(2)}) collective-permute-start(f32[1,8,96,128]{3,2,1,0:T(8,128)S(1)} %get-tuple-element.77), channel_id=1, source_target_pairs={{8,0},{16,8},{24,16},{9,1},{17,9},{25,17},{10,2},{18,10},{26,18},{... | collective-permute-start | bytes 1179656 | tf_op jit(solution)/shard_map/ppermute | solution.py:19
  277.6 39.7 %collective-permute-start.21 = (f32[18,1,96,128]{3,2,1,0:T(8,128)S(1)}, f32[18,1,96,128]{3,2,1,0:T(8,128)S(1)}, u32[]{:S(2)}, u32[]{:S(2)}) collective-permute-start(f32[18,1,96,128]{3,2,1,0:T(8,128)S(1)} %get-tuple-element.64), channel_id=1, source_target_pairs={{0,2},{2,4},{4,6},{1,3},{3,5},{5,7},{8,10},{10,12},{12,14},{9,11},... | collective-permute-start | bytes 2654216 | tf_op jit(solution)/shard_map/ppermute | solution.py:17
  278.9 38.4 %collective-permute-start.20 = (f32[18,1,96,128]{3,2,1,0:T(8,128)S(1)}, f32[18,1,96,128]{3,2,1,0:T(8,128)S(1)}, u32[]{:S(2)}, u32[]{:S(2)}) collective-permute-start(f32[18,1,96,128]{3,2,1,0:T(8,128)S(1)} %get-tuple-element.65), channel_id=1, source_target_pairs={{2,0},{4,2},{6,4},{3,1},{5,3},{7,5},{10,8},{12,10},{14,12},{11,9},... | collective-permute-start | bytes 2654216 | tf_op jit(solution)/shard_map/ppermute | solution.py:19
  317.3 1.0 copy-start.9
  318.3 4.4 collective-permute-start.22
  319.6 4.0 collective-permute-start.23
  348.7 57.9 %copy-start.2 = (f32[16,8,96,128]{3,2,1,0:T(8,128)S(1)}, f32[16,8,96,128]{3,2,1,0:T(8,128)}, u32[]{:S(2)}) copy-start(f32[16,8,96,128]{3,2,1,0:T(8,128)} %multiply_add_fusion.2) | copy-start | bytes 18874372
  350.1 13.4 %collective-permute-start.25 = (f32[1,8,96,128]{3,2,1,0:T(8,128)S(1)}, f32[1,8,96,128]{3,2,1,0:T(8,128)S(1)}, u32[]{:S(2)}, u32[]{:S(2)}) collective-permute-start(f32[1,8,96,128]{3,2,1,0:T(8,128)S(1)} %get-tuple-element.74), channel_id=1, source_target_pairs={{0,8},{8,16},{16,24},{1,9},{9,17},{17,25},{2,10},{10,18},{18,26},{... | collective-permute-start | bytes 1179656 | tf_op jit(solution)/shard_map/ppermute | solution.py:17
  352.1 13.3 %collective-permute-start.24 = (f32[1,8,96,128]{3,2,1,0:T(8,128)S(1)}, f32[1,8,96,128]{3,2,1,0:T(8,128)S(1)}, u32[]{:S(2)}, u32[]{:S(2)}) collective-permute-start(f32[1,8,96,128]{3,2,1,0:T(8,128)S(1)} %get-tuple-element.75), channel_id=1, source_target_pairs={{8,0},{16,8},{24,16},{9,1},{17,9},{25,17},{10,2},{18,10},{26,18},{... | collective-permute-start | bytes 1179656 | tf_op jit(solution)/shard_map/ppermute | solution.py:19
  366.9 39.7 %collective-permute-start.27 = (f32[18,1,96,128]{3,2,1,0:T(8,128)S(1)}, f32[18,1,96,128]{3,2,1,0:T(8,128)S(1)}, u32[]{:S(2)}, u32[]{:S(2)}) collective-permute-start(f32[18,1,96,128]{3,2,1,0:T(8,128)S(1)} %get-tuple-element.62), channel_id=1, source_target_pairs={{0,2},{2,4},{4,6},{1,3},{3,5},{5,7},{8,10},{10,12},{12,14},{9,11},... | collective-permute-start | bytes 2654216 | tf_op jit(solution)/shard_map/ppermute | solution.py:17
  368.2 38.4 %collective-permute-start.26 = (f32[18,1,96,128]{3,2,1,0:T(8,128)S(1)}, f32[18,1,96,128]{3,2,1,0:T(8,128)S(1)}, u32[]{:S(2)}, u32[]{:S(2)}) collective-permute-start(f32[18,1,96,128]{3,2,1,0:T(8,128)S(1)} %get-tuple-element.63), channel_id=1, source_target_pairs={{2,0},{4,2},{6,4},{3,1},{5,3},{7,5},{10,8},{12,10},{14,12},{11,9},... | collective-permute-start | bytes 2654216 | tf_op jit(solution)/shard_map/ppermute | solution.py:19
  406.6 1.0 copy-start.10
  407.6 4.6 collective-permute-start.28
  408.9 4.0 collective-permute-start.29
  437.7 57.9 %copy-start.3 = (f32[16,8,96,128]{3,2,1,0:T(8,128)S(1)}, f32[16,8,96,128]{3,2,1,0:T(8,128)}, u32[]{:S(2)}) copy-start(f32[16,8,96,128]{3,2,1,0:T(8,128)} %multiply_add_fusion.1) | copy-start | bytes 18874372
  439.1 13.4 %collective-permute-start.31 = (f32[1,8,96,128]{3,2,1,0:T(8,128)S(1)}, f32[1,8,96,128]{3,2,1,0:T(8,128)S(1)}, u32[]{:S(2)}, u32[]{:S(2)}) collective-permute-start(f32[1,8,96,128]{3,2,1,0:T(8,128)S(1)} %get-tuple-element.72), channel_id=1, source_target_pairs={{0,8},{8,16},{16,24},{1,9},{9,17},{17,25},{2,10},{10,18},{18,26},{... | collective-permute-start | bytes 1179656 | tf_op jit(solution)/shard_map/ppermute | solution.py:17
  441.1 13.3 %collective-permute-start.30 = (f32[1,8,96,128]{3,2,1,0:T(8,128)S(1)}, f32[1,8,96,128]{3,2,1,0:T(8,128)S(1)}, u32[]{:S(2)}, u32[]{:S(2)}) collective-permute-start(f32[1,8,96,128]{3,2,1,0:T(8,128)S(1)} %get-tuple-element.73), channel_id=1, source_target_pairs={{8,0},{16,8},{24,16},{9,1},{17,9},{25,17},{10,2},{18,10},{26,18},{... | collective-permute-start | bytes 1179656 | tf_op jit(solution)/shard_map/ppermute | solution.py:19
  455.9 39.7 %collective-permute-start.33 = (f32[18,1,96,128]{3,2,1,0:T(8,128)S(1)}, f32[18,1,96,128]{3,2,1,0:T(8,128)S(1)}, u32[]{:S(2)}, u32[]{:S(2)}) collective-permute-start(f32[18,1,96,128]{3,2,1,0:T(8,128)S(1)} %get-tuple-element.60), channel_id=1, source_target_pairs={{0,2},{2,4},{4,6},{1,3},{3,5},{5,7},{8,10},{10,12},{12,14},{9,11},... | collective-permute-start | bytes 2654216 | tf_op jit(solution)/shard_map/ppermute | solution.py:17
  457.2 38.4 %collective-permute-start.32 = (f32[18,1,96,128]{3,2,1,0:T(8,128)S(1)}, f32[18,1,96,128]{3,2,1,0:T(8,128)S(1)}, u32[]{:S(2)}, u32[]{:S(2)}) collective-permute-start(f32[18,1,96,128]{3,2,1,0:T(8,128)S(1)} %get-tuple-element.61), channel_id=1, source_target_pairs={{2,0},{4,2},{6,4},{3,1},{5,3},{7,5},{10,8},{12,10},{14,12},{11,9},... | collective-permute-start | bytes 2654216 | tf_op jit(solution)/shard_map/ppermute | solution.py:19
  495.6 1.0 copy-start.11
  496.6 4.4 collective-permute-start.34
  497.9 4.0 collective-permute-start.35
  530.8 2.7 copy-start.6
Sparse Core Ops, SparseCore 0:
  534.6 61.6 all-gather.2
where the time goes:
time: 615 us; the launch traced here: 614 us
  waiting for transfers between devices  232 us (38%)
  starting transfers between devices  174 us (28%)
  other arithmetic  172 us (28%)
  local copies, waits for them, and re-layouts  20.5 us (3%)
  between operations  14.8 us (2%)
    ppermute x18, waiting for transfers between devices, with_halo(): lax.ppermute(tail, axis, [(i, (i + 1) % count) for i in range(ends)])  159 us
    add x6, other arithmetic, single_update(): middle - scaled_wind_north * slopes[0] - scaled_wind_east * slopes[1]  150 us
    ppermute x18, starting transfers between devices, with_halo(): lax.ppermute(head, axis, [((i + 1) % count, i) for i in range(ends)])  132 us
    all_gather x1, waiting for transfers between devices, entering(): gathered = lax.all_gather(part, axis)  61.9 us
    ppermute x18, starting transfers between devices, with_halo(): lax.ppermute(tail, axis, [(i, (i + 1) % count) for i in range(ends)])  42 us
  transfers between devices with their start and end apart: 37, of which 24 were waited for; matrix products, arithmetic and copies ran while one was open for 1% of the time, Pallas kernels for 0%

commit v1 on v0

v1 whole, which is shorter than its diff:
```python
import functools

import jax
import jax.numpy as jnp
from jax import lax
from jax.experimental import pallas as pl
from jax.experimental.pallas import tpu as pltpu
from jax.sharding import PartitionSpec as P

STEPS = 6
RATE = 0.05
LAG = 1
TOTAL_LAG = 4
RELAY = False
RELAY_FIRST_DIM = True
MESH = pl.DeviceIdType.MESH


def relay_routes(mesh):
    if not RELAY:
        return ()
    row = mesh.devices[0, :, 0]
    spots = [getattr(device, "coords", None) for device in row]
    if any(spot is None for spot in spots):
        return ()
    spots = [tuple(spot) for spot in spots]
    routes = []
    for low in range(len(spots) - 1):
        for source, target, side in ((low, low + 1, 0), (low + 1, low, 1)):
            a, b = spots[source], spots[target]
            differ = [d for d in range(3) if a[d] != b[d]]
            if len(differ) != 2:
                continue
            keep, change = differ if RELAY_FIRST_DIM else differ[::-1]
            corner = list(a)
            corner[change] = b[change]
            if tuple(corner) in spots:
                routes.append((source, spots.index(tuple(corner)), target, side))
    return tuple(routes)


def march(routes, sizes, heat, north, east, vert, end_out, enter_out,
          T, W, zh, zs, tot, ent, rbuf,
          load_sem, xs_sem, xr_sem, ys_sem, yr_sem, zs_sem, zr_sem,
          rs_in_sem, rr_sem, rs_sem, ts_sem, tr_sem, out_sem, enter_sem):
    lats, lons, levs = sizes
    Y, X, Z, L = heat.shape
    pairs = Y // 2
    lat, lon, lev = (lax.axis_index(a) for a in ("lat", "lon", "lev"))
    winds = (north, east, vert)

    def remote(src, dst, send, recv, where):
        return pltpu.make_async_remote_copy(
            src_ref=src, dst_ref=dst, send_sem=send, recv_sem=recv,
            device_id=where, device_id_type=MESH)

    def load(j, k):
        if k == 3:
            return pltpu.make_async_copy(heat.at[j], T.at[0, 1 + j, pl.ds(1, X)], load_sem.at[3, j])
        return pltpu.make_async_copy(winds[k].at[j], W.at[k, j], load_sem.at[k, j])

    def start_loads(p, _):
        for k in range(3):
            load(p, k).start()
            load(Y - 1 - p, k).start()
        return 0

    def start_heat(j, _):
        load(j, 3).start()
        return 0

    lax.fori_loop(0, Y, start_heat, 0)
    lax.fori_loop(0, pairs, start_loads, 0)

    @pl.when(lon == 0)
    def _():
        T[:, pl.ds(1, Y), 0] = jnp.zeros((2, Y, Z, L), jnp.float32)

    @pl.when(lon == lons - 1)
    def _():
        T[:, pl.ds(1, Y), X + 1] = jnp.zeros((2, Y, Z, L), jnp.float32)

    @pl.when(lat == 0)
    def _():
        T[:, 0, pl.ds(1, X)] = jnp.zeros((2, X, Z, L), jnp.float32)

    @pl.when(lat == lats - 1)
    def _():
        T[:, Y + 1, pl.ds(1, X)] = jnp.zeros((2, X, Z, L), jnp.float32)

    @pl.when(lev == 0)
    def _():
        zh[:, 0] = jnp.zeros((2, Y, X, L), jnp.float32)

    @pl.when(lev == levs - 1)
    def _():
        zh[:, 1] = jnp.zeros((2, Y, X, L), jnp.float32)

    barrier = pltpu.get_barrier_semaphore()
    expected = jnp.int32(0)
    for axis, place, count in (("lat", lat, lats), ("lon", lon, lons), ("lev", lev, levs)):
        for cond, other in ((place > 0, place - 1), (place < count - 1, place + 1)):
            @pl.when(cond)
            def _(axis=axis, other=other):
                pl.semaphore_signal(barrier, inc=1, device_id={axis: other}, device_id_type=MESH)
            expected = expected + jnp.where(cond, 1, 0)
    met = set()
    for source, relay, target, _ in routes:
        for a, b in ((source, relay), (relay, target)):
            link = (min(a, b), max(a, b))
            if link[1] - link[0] == 1 or link in met:
                continue
            met.add(link)
            for me, other in (link, link[::-1]):
                @pl.when(lon == me)
                def _(other=other):
                    pl.semaphore_signal(barrier, inc=1, device_id={"lon": jnp.int32(other)}, device_id_type=MESH)
                expected = expected + jnp.where(lon == me, 1, 0)
    pl.semaphore_wait(barrier, expected)

    def x_copy(slot, side, j, src):
        land = 0 if side == 0 else X + 1
        other = lon + 1 if side == 0 else lon - 1
        return remote(src, T.at[slot, 1 + j, land], xs_sem.at[slot, side, j],
                      xr_sem.at[slot, side, j], {"lon": other})

    def has_target(side):
        return lon < lons - 1 if side == 0 else lon > 0

    def has_source(side):
        return lon > 0 if side == 0 else lon < lons - 1

    def on_route(side, relayed):
        hit = False
        if relayed:
            for source, _, _, s in routes:
                if s == side:
                    hit = jnp.logical_or(hit, lon == source)
        return hit

    def send_x(step, slot, j, p, relayed, srcs):
        for side in (0, 1):
            routed = on_route(side, relayed)

            @pl.when(jnp.logical_and(has_target(side), jnp.logical_not(routed)))
            def _(side=side):
                x_copy(slot, side, j, srcs[side]).start()

        if relayed:
            for number, (source, relay, target, side) in enumerate(routes):
                @pl.when(lon == source)
                def _(relay=relay, side=side):
                    remote(srcs[side], rbuf.at[step, p], xs_sem.at[slot, side, j],
                           rr_sem.at[step, p], {"lon": jnp.int32(relay)}).start()

    def wait_send_x(slot, j):
        for side in (0, 1):
            @pl.when(has_target(side))
            def _(side=side):
                x_copy(slot, side, j, T.at[slot, 1 + j, X if side == 0 else 1]).wait_send()

    def wait_recv_x(slot, j):
        for side in (0, 1):
            @pl.when(has_source(side))
            def _(side=side):
                x_copy(slot, side, j, T.at[slot, 1 + j, X if side == 0 else 1]).wait_recv()

    def relay_copy(step, p, target, side):
        slot = lax.rem(step, 2)
        j = Y - 1 - p
        land = 0 if side == 0 else X + 1
        return remote(rbuf.at[step, p], T.at[slot, 1 + j, land], rs_sem.at[step, p],
                      xr_sem.at[slot, side, j], {"lon": jnp.int32(target)})

    def do_relay(step, p):
        for source, relay, target, side in routes:
            @pl.when(lon == relay)
            def _(target=target, side=side):
                remote(rbuf.at[step, p], rbuf.at[step, p], rs_in_sem.at[0],
                       rr_sem.at[step, p], {"lon": jnp.int32(target)}).wait_recv()
                relay_copy(step, p, target, side).start()

    def y_copy(slot, side):
        if side == 0:
            return remote(T.at[slot, Y, pl.ds(1, X)], T.at[slot, 0, pl.ds(1, X)],
                          ys_sem.at[slot, 0], yr_sem.at[slot, 0], {"lat": lat + 1})
        return remote(T.at[slot, 1, pl.ds(1, X)], T.at[slot, Y + 1, pl.ds(1, X)],
                      ys_sem.at[slot, 1], yr_sem.at[slot, 1], {"lat": lat - 1})

    def y_target(side):
        return lat < lats - 1 if side == 0 else lat > 0

    def y_source(side):
        return lat > 0 if side == 0 else lat < lats - 1

    def z_copy(slot, side, j):
        other = lev + 1 if side == 0 else lev - 1
        return remote(zs.at[slot, side, j], zh.at[slot, side, j], zs_sem.at[slot, side, j],
                      zr_sem.at[slot, side, j], {"lev": other})

    def z_target(side):
        return lev < levs - 1 if side == 0 else lev > 0

    def z_source(side):
        return lev > 0 if side == 0 else lev < levs - 1

    def send_z(slot, j):
        for side in (0, 1):
            @pl.when(z_target(side))
            def _(side=side):
                z_copy(slot, side, j).start()

    def wait_send_z(slot, j):
        for side in (0, 1):
            @pl.when(z_target(side))
            def _(side=side):
                z_copy(slot, side, j).wait_send()

    def wait_recv_z(slot, j):
        for side in (0, 1):
            @pl.when(z_source(side))
            def _(side=side):
                z_copy(slot, side, j).wait_recv()

    def first_x(p, _):
        for j, relayed in ((p, False), (Y - 1 - p, True)):
            send_x(0, 0, j, p, relayed, (heat.at[j, X - 1], heat.at[j, 0]))
        return 0

    lax.fori_loop(0, pairs, first_x, 0)

    def wait_heat(j, _):
        load(j, 3).wait()
        return 0

    lax.fori_loop(0, Y, wait_heat, 0)
    for side in (0, 1):
        @pl.when(y_target(side))
        def _(side=side):
            y_copy(0, side).start()

    def first_z(j, _):
        for x in range(X):
            zs[0, 0, j, pl.ds(x, 1)] = T[0, 1 + j, 1 + x, pl.ds(Z - 1, 1)]
            zs[0, 1, j, pl.ds(x, 1)] = T[0, 1 + j, 1 + x, pl.ds(0, 1)]
        return 0

    lax.fori_loop(0, Y, first_z, 0)

    def first_z_send(j, _):
        send_z(0, j)
        return 0

    lax.fori_loop(0, Y, first_z_send, 0)

    level = lax.broadcasted_iota(jnp.int32, (Z, L), 0)

    def update(old, j, with_total):
        new = 1 - old
        total = None
        for x in range(X):
            c = T[old, 1 + j, 1 + x]
            ym, yp = T[old, j, 1 + x], T[old, j + 2, 1 + x]
            xm, xp = T[old, 1 + j, x], T[old, 1 + j, x + 2]
            zm = jnp.where(level == 0, zh[old, 0, j, pl.ds(x, 1)], pltpu.roll(c, 1, 0))
            zp = jnp.where(level == Z - 1, zh[old, 1, j, pl.ds(x, 1)], pltpu.roll(c, Z - 1, 0))
            spread = ym + yp + xm + xp + zm + zp - 6.0 * c
            value = (c - W[0, j, x] * (yp - ym) - W[1, j, x] * (xp - xm)
                     - W[2, j, x] * (zp - zm) + RATE * spread)
            T[new, 1 + j, 1 + x] = value
            if not with_total:
                zs[new, 0, j, pl.ds(x, 1)] = value[Z - 1:Z]
                zs[new, 1, j, pl.ds(x, 1)] = value[0:1]
            elif total is None:
                total = value
            else:
                total = total + value
        if with_total:
            tot[j] = total

    def arrivals(old, j, p, edge_side):
        wait_recv_x(old, j)
        wait_recv_z(old, j)

        @pl.when(jnp.logical_and(p == 0, y_source(edge_side)))
        def _():
            y_copy(old, edge_side).wait_recv()

    def departures(slot, j, p, edge_side):
        wait_send_x(slot, j)
        wait_send_z(slot, j)

        @pl.when(jnp.logical_and(p == 0, y_target(edge_side)))
        def _():
            y_copy(slot, edge_side).wait_send()

    def one_pair(q, _):
        step = q // pairs
        p = lax.rem(q, pairs)
        old = lax.rem(step, 2)
        new = 1 - old

        @pl.when(step == 0)
        def _():
            do_relay(0, p)
            for k in range(3):
                load(p, k).wait()
                load(Y - 1 - p, k).wait()

        for j, edge_side, relayed in ((p, 0, False), (Y - 1 - p, 1, True)):
            arrivals(old, j, p, edge_side)

            @pl.when(step > 0)
            def _(j=j, edge_side=edge_side):
                departures(new, j, p, 1 - edge_side)

            update(old, j, False)
            send_x(step + 1, new, j, p, relayed, (T.at[new, 1 + j, X], T.at[new, 1 + j, 1]))
            send_z(new, j)

            @pl.when(jnp.logical_and(p == 0, y_target(1 - edge_side)))
            def _(edge_side=edge_side):
                y_copy(new, 1 - edge_side).start()

        late = q - LAG

        @pl.when(late >= 0)
        def _():
            do_relay(late // pairs + 1, lax.rem(late, pairs))

        return 0

    lax.fori_loop(0, (STEPS - 1) * pairs, one_pair, 0)

    old = (STEPS - 1) % 2
    new = 1 - old

    def out_copy(j):
        return pltpu.make_async_copy(T.at[new, 1 + j, pl.ds(1, X)], end_out.at[j], out_sem.at[j])

    def t_copy(j):
        return remote(tot.at[j], ent.at[j], ts_sem.at[j], tr_sem.at[j], {"lon": lon + 1})

    def enter_copy(j):
        return pltpu.make_async_copy(ent.at[j], enter_out.at[j], enter_sem.at[j])

    def pass_total(p):
        for j in (p, Y - 1 - p):
            @pl.when(lon > 0)
            def _(j=j):
                t_copy(j).wait_recv()

                @pl.when(lon < lons - 1)
                def _():
                    tot[j] = tot[j] + ent[j]
                    t_copy(j).start()

            enter_copy(j).start()

    def clear_enter(j, _):
        ent[j] = jnp.zeros((Z, L), jnp.float32)
        return 0

    @pl.when(lon == 0)
    def _():
        lax.fori_loop(0, Y, clear_enter, 0)

    def leftover(p, _):
        do_relay(STEPS - 1, p)
        return 0

    lax.fori_loop(pairs - LAG, pairs, leftover, 0)

    def last_pair(p, _):
        for j, edge_side in ((p, 0), (Y - 1 - p, 1)):
            arrivals(old, j, p, edge_side)
            departures(new, j, p, 1 - edge_side)
            update(old, j, True)
        for j in (p, Y - 1 - p):
            @pl.when(jnp.logical_and(lon == 0, lons > 1))
            def _(j=j):
                t_copy(j).start()

            out_copy(j).start()

        @pl.when(p >= TOTAL_LAG)
        def _():
            pass_total(p - TOTAL_LAG)

        return 0

    lax.fori_loop(0, pairs, last_pair, 0)

    def last_totals(p, _):
        pass_total(p)
        return 0

    lax.fori_loop(max(pairs - TOTAL_LAG, 0), pairs, last_totals, 0)

    def drain(j, _):
        wait_send_x(old, j)
        wait_send_z(old, j)

        @pl.when(lon < lons - 1)
        def _():
            t_copy(j).wait_send()

        out_copy(j).wait()
        enter_copy(j).wait()
        return 0

    lax.fori_loop(0, Y, drain, 0)
    for side in (0, 1):
        @pl.when(y_target(side))
        def _(side=side):
            y_copy(old, side).wait_send()

    for source, relay, target, side in routes:
        def close(p, _, target=target, side=side):
            for step in range(STEPS):
                relay_copy(step, p, target, side).wait_send()
            return 0

        @pl.when(lon == relay)
        def _(close=close):
            lax.fori_loop(0, pairs, close, 0)


def integrate(scale, end_ref, enter_ref, acc_ref, copy_ref):
    X = end_ref.shape[1]
    running = enter_ref[0]
    for x in range(X):
        value = end_ref[0, x]
        copy_ref[0, x] = value
        running = running + value
        acc_ref[0, x] = running * scale


def per_device(routes, sizes, heat, north, east, vert):
    Y, X, Z, L = heat.shape
    pairs = Y // 2
    f32 = jnp.float32
    any_spec = pl.BlockSpec(memory_space=pl.ANY)
    dma = pltpu.SemaphoreType.DMA
    relay_rows = (STEPS, pairs) if routes else (1, 1)
    end, enter = pl.pallas_call(
        functools.partial(march, routes, sizes),
        out_shape=(jax.ShapeDtypeStruct((Y, X, Z, L), f32), jax.ShapeDtypeStruct((Y, Z, L), f32)),
        in_specs=[any_spec] * 4,
        out_specs=(any_spec, any_spec),
        scratch_shapes=[
            pltpu.VMEM((2, Y + 2, X + 2, Z, L), f32),
            pltpu.VMEM((3, Y, X, Z, L), f32),
            pltpu.VMEM((2, 2, Y, X, L), f32),
            pltpu.VMEM((2, 2, Y, X, L), f32),
            pltpu.VMEM((Y, Z, L), f32),
            pltpu.VMEM((Y, Z, L), f32),
            pltpu.VMEM(relay_rows + (Z, L), f32),
            dma((4, Y)),
            dma((2, 2, Y)), dma((2, 2, Y)),
            dma((2, 2)), dma((2, 2)),
            dma((2, 2, Y)), dma((2, 2, Y)),
            dma((1,)), dma(relay_rows), dma(relay_rows),
            dma((Y,)), dma((Y,)), dma((Y,)), dma((Y,)),
        ],
        compiler_params=pltpu.CompilerParams(
            collective_id=0, has_side_effects=True, vmem_limit_bytes=62 * 1024 * 1024),
        name="march",
    )(heat, north, east, vert)
    row = pl.BlockSpec((1, X, Z, L), lambda j: (j, 0, 0, 0))
    return pl.pallas_call(
        functools.partial(integrate, 1.0 / (X * sizes[1])),
        grid=(Y,),
        in_specs=[row, pl.BlockSpec((1, Z, L), lambda j: (j, 0, 0))],
        out_specs=(row, row),
        out_shape=(jax.ShapeDtypeStruct((Y, X, Z, L), f32),) * 2,
        name="integrate",
    )(end, enter)


def solution(mesh):
    spec = P("lat", "lon", "lev", None)
    sizes = tuple(mesh.shape[a] for a in ("lat", "lon", "lev"))
    return jax.shard_map(
        functools.partial(per_device, relay_routes(mesh), sizes),
        mesh=mesh, in_specs=(spec,) * 4, out_specs=(spec, spec), check_vma=False)
```

time: 615 us -> 243 us (0.40)
  Pallas kernels: 0 us -> 242 us
  waiting for transfers between devices: 232 us -> 0 us
  starting transfers between devices: 174 us -> 0 us
  other arithmetic: 172 us -> 0 us
  local copies, waits for them, and re-layouts: 20.5 us -> 0 us
  between operations: 14.8 us -> 0.64 us
    pallas_call x0 -> x2, Pallas kernels: none -> 242 us  [the longest x1 230 us: per_device(): pl.pallas_call(functools.partial(march, routes, sizes), out_shape=(jax.Sh...]
    ppermute x36 -> x0, starting transfers between devices: 174 us -> none  [the longest x18 132 us: with_halo(): lax.ppermute(head, axis, [((i + 1) % count, i) for i in range(ends)])]
    ppermute x36 -> x0, waiting for transfers between devices: 170 us -> none  [the longest x18 159 us: with_halo(): lax.ppermute(tail, axis, [(i, (i + 1) % count) for i in range(ends)])]
    add x9 -> x0, other arithmetic: 154 us -> none  [the longest x6 150 us: single_update(): middle - scaled_wind_north * slopes[0] - scaled_wind_east * slopes[1]]
    all_gather x1 -> x0, waiting for transfers between devices: 61.9 us -> none  [entering(): gathered = lax.all_gather(part, axis)]
    unnamed x34 -> x0, local copies, waits for them, and re-layouts: 10.3 us -> none
    slice x20 -> x0, local copies, waits for them, and re-layouts: 8.97 us -> none  [the longest x12 6.79 us: with_halo(): lax.slice_in_dim(cells, cells.shape[dim] - width, cells.shape[dim], axis=...]
    concatenate x11 -> x0, other arithmetic: 8.33 us -> none  [with_halo(): jnp.concatenate([lax.ppermute(tail, axis, [(i, (i + 1) % count) for i in...]
  transfers between devices with their start and end apart: 37 -> 0, of which waited for: 24 -> 0; matrix products, arithmetic and copies ran while one was open for 1% -> 0% of each run, Pallas kernels for 0% -> 0%
where the time goes in v1:
time: 243 us
  Pallas kernels  242 us (100%)
    pallas_call x1, Pallas kernels, per_device(): pl.pallas_call(functools.partial(march, routes, sizes), out_shape=(jax.Sh...  230 us
    pallas_call x1, Pallas kernels, per_device(): pl.pallas_call(functools.partial(integrate, 1.0 / (X * sizes[1])), grid=(...  12.1 us

profile of v1, /device:TPU:22, one launch (start us, length us, event | category | flops | bytes accessed | tf_op | source)
XLA Modules:
  0.0 242.7 jit_solution(4142976208303877440)
XLA Ops:
  0.6 229.9 %march.1 = (f32[16,8,96,128]{3,2,1,0:T(8,128)}, f32[16,96,128]{2,1,0:T(8,128)}) custom-call(f32[16,8,96,128]{3,2,1,0:T(8,128)} %heat.1, f32[16,8,96,128]{3,2,1,0:T(8,128)} %north.1, f32[16,8,96,128]{3,2,1,0:T(8,128)} %east.1, f32[16,8,96,128]{3,2,1,0:T(8,128)} %vert.1), custom_call_target="tpu_custom_call" | custom-call | tf_op jit(solution)/shard_map/march/pallas_call | solution.py:446
  230.6 12.1 %integrate.1 = (f32[16,8,96,128]{3,2,1,0:T(8,128)}, f32[16,8,96,128]{3,2,1,0:T(8,128)}) custom-call(f32[16,8,96,128]{3,2,1,0:T(8,128)} %get-tuple-element.4.end_ref, f32[16,96,128]{2,1,0:T(8,128)} %get-tuple-element.5.enter_ref), custom_call_target="tpu_custom_call" | custom-call | tf_op jit(solution)/shard_map/integrate/pallas_call | solution.py:471

commit v2 on v1

--- a/solution.py
+++ b/solution.py
@@ -11,7 +11,7 @@
 RATE = 0.05
 LAG = 1
 TOTAL_LAG = 4
-RELAY = False
+RELAY = True
 RELAY_FIRST_DIM = True
 MESH = pl.DeviceIdType.MESH
 

time: 243 us -> 197 us (0.81)
  Pallas kernels: 242 us -> 196 us
    pallas_call x1, Pallas kernels: 230 us -> 184 us  [per_device(): pl.pallas_call(functools.partial(march, routes, sizes), out_shape=(jax.Sh...]
where the time goes in v2:
time: 197 us; the launch traced here: 196 us
  Pallas kernels  196 us (99%)
    pallas_call x1, Pallas kernels, per_device(): pl.pallas_call(functools.partial(march, routes, sizes), out_shape=(jax.Sh...  184 us
    pallas_call x1, Pallas kernels, per_device(): pl.pallas_call(functools.partial(integrate, 1.0 / (X * sizes[1])), grid=(...  12.1 us

profile of v2, /device:TPU:22, one launch (start us, length us, event | category | flops | bytes accessed | tf_op | source)
XLA Modules:
  0.0 196.4 jit_solution(16291998986635249888)
XLA Ops:
  0.6 183.7 %march.1 = (f32[16,8,96,128]{3,2,1,0:T(8,128)}, f32[16,96,128]{2,1,0:T(8,128)}) custom-call(f32[16,8,96,128]{3,2,1,0:T(8,128)} %heat.1, f32[16,8,96,128]{3,2,1,0:T(8,128)} %north.1, f32[16,8,96,128]{3,2,1,0:T(8,128)} %east.1, f32[16,8,96,128]{3,2,1,0:T(8,128)} %vert.1), custom_call_target="tpu_custom_call" | custom-call | tf_op jit(solution)/shard_map/march/pallas_call | solution.py:446
  184.3 12.1 %integrate.1 = (f32[16,8,96,128]{3,2,1,0:T(8,128)}, f32[16,8,96,128]{3,2,1,0:T(8,128)}) custom-call(f32[16,8,96,128]{3,2,1,0:T(8,128)} %get-tuple-element.4.end_ref, f32[16,96,128]{2,1,0:T(8,128)} %get-tuple-element.5.enter_ref), custom_call_target="tpu_custom_call" | custom-call | tf_op jit(solution)/shard_map/integrate/pallas_call | solution.py:471

commit v3 on v2

--- a/solution.py
+++ b/solution.py
@@ -105,17 +105,19 @@
                 pl.semaphore_signal(barrier, inc=1, device_id={axis: other}, device_id_type=MESH)
             expected = expected + jnp.where(cond, 1, 0)
     met = set()
+    links = [(low, low + 2) for low in range(lons - 2)]
     for source, relay, target, _ in routes:
-        for a, b in ((source, relay), (relay, target)):
-            link = (min(a, b), max(a, b))
-            if link[1] - link[0] == 1 or link in met:
-                continue
-            met.add(link)
-            for me, other in (link, link[::-1]):
-                @pl.when(lon == me)
-                def _(other=other):
-                    pl.semaphore_signal(barrier, inc=1, device_id={"lon": jnp.int32(other)}, device_id_type=MESH)
-                expected = expected + jnp.where(lon == me, 1, 0)
+        links += [(source, relay), (relay, target)]
+    for a, b in links:
+        link = (min(a, b), max(a, b))
+        if link[1] - link[0] == 1 or link in met:
+            continue
+        met.add(link)
+        for me, other in (link, link[::-1]):
+            @pl.when(lon == me)
+            def _(other=other):
+                pl.semaphore_signal(barrier, inc=1, device_id={"lon": jnp.int32(other)}, device_id_type=MESH)
+            expected = expected + jnp.where(lon == me, 1, 0)
     pl.semaphore_wait(barrier, expected)
 
     def x_copy(slot, side, j, src):
@@ -276,7 +278,7 @@
             else:
                 total = total + value
         if with_total:
-            tot[j] = total
+            tot[0, j] = total
 
     def arrivals(old, j, p, edge_side):
         wait_recv_x(old, j)
@@ -338,27 +340,35 @@
     def out_copy(j):
         return pltpu.make_async_copy(T.at[new, 1 + j, pl.ds(1, X)], end_out.at[j], out_sem.at[j])
 
-    def t_copy(j):
-        return remote(tot.at[j], ent.at[j], ts_sem.at[j], tr_sem.at[j], {"lon": lon + 1})
+    def near_copy(j):
+        return remote(tot.at[0, j], ent.at[0, j], ts_sem.at[0, j], tr_sem.at[0, j], {"lon": lon + 1})
+
+    def far_copy(j, which):
+        return remote(tot.at[which, j], ent.at[1, j], ts_sem.at[1, j], tr_sem.at[1, j], {"lon": lon + 2})
 
     def enter_copy(j):
-        return pltpu.make_async_copy(ent.at[j], enter_out.at[j], enter_sem.at[j])
+        return pltpu.make_async_copy(ent.at[0, j], enter_out.at[j], enter_sem.at[j])
 
     def pass_total(p):
         for j in (p, Y - 1 - p):
             @pl.when(lon > 0)
             def _(j=j):
-                t_copy(j).wait_recv()
-
-                @pl.when(lon < lons - 1)
-                def _():
-                    tot[j] = tot[j] + ent[j]
-                    t_copy(j).start()
+                near_copy(j).wait_recv()
+
+            @pl.when(lon > 1)
+            def _(j=j):
+                far_copy(j, 1).wait_recv()
+                ent[0, j] = ent[0, j] + ent[1, j]
+
+            @pl.when(jnp.logical_and(lon > 0, lon < lons - 2))
+            def _(j=j):
+                tot[1, j] = tot[0, j] + ent[0, j]
+                far_copy(j, 1).start()
 
             enter_copy(j).start()
 
     def clear_enter(j, _):
-        ent[j] = jnp.zeros((Z, L), jnp.float32)
+        ent[0, j] = jnp.zeros((Z, L), jnp.float32)
         return 0
 
     @pl.when(lon == 0)
@@ -377,9 +387,13 @@
             departures(new, j, p, 1 - edge_side)
             update(old, j, True)
         for j in (p, Y - 1 - p):
-            @pl.when(jnp.logical_and(lon == 0, lons > 1))
+            @pl.when(jnp.logical_and(lon == 0, lons > 2))
             def _(j=j):
-                t_copy(j).start()
+                far_copy(j, 0).start()
+
+            @pl.when(lon < lons - 1)
+            def _(j=j):
+                near_copy(j).start()
 
             out_copy(j).start()
 
@@ -403,7 +417,11 @@
 
         @pl.when(lon < lons - 1)
         def _():
-            t_copy(j).wait_send()
+            near_copy(j).wait_send()
+
+        @pl.when(lon < lons - 2)
+        def _():
+            far_copy(j, 1).wait_send()
 
         out_copy(j).wait()
         enter_copy(j).wait()
@@ -443,6 +461,8 @@
     any_spec = pl.BlockSpec(memory_space=pl.ANY)
     dma = pltpu.SemaphoreType.DMA
     relay_rows = (STEPS, pairs) if routes else (1, 1)
+    block = 4 * (Y + 2) * (X + 2) * Z * L
+    grant = 5 * block + block // 8
     end, enter = pl.pallas_call(
         functools.partial(march, routes, sizes),
         out_shape=(jax.ShapeDtypeStruct((Y, X, Z, L), f32), jax.ShapeDtypeStruct((Y, Z, L), f32)),
@@ -453,18 +473,18 @@
             pltpu.VMEM((3, Y, X, Z, L), f32),
             pltpu.VMEM((2, 2, Y, X, L), f32),
             pltpu.VMEM((2, 2, Y, X, L), f32),
-            pltpu.VMEM((Y, Z, L), f32),
-            pltpu.VMEM((Y, Z, L), f32),
+            pltpu.VMEM((2, Y, Z, L), f32),
+            pltpu.VMEM((2, Y, Z, L), f32),
             pltpu.VMEM(relay_rows + (Z, L), f32),
             dma((4, Y)),
             dma((2, 2, Y)), dma((2, 2, Y)),
             dma((2, 2)), dma((2, 2)),
             dma((2, 2, Y)), dma((2, 2, Y)),
             dma((1,)), dma(relay_rows), dma(relay_rows),
-            dma((Y,)), dma((Y,)), dma((Y,)), dma((Y,)),
+            dma((2, Y)), dma((2, Y)), dma((Y,)), dma((Y,)),
         ],
         compiler_params=pltpu.CompilerParams(
-            collective_id=0, has_side_effects=True, vmem_limit_bytes=62 * 1024 * 1024),
+            collective_id=0, has_side_effects=True, vmem_limit_bytes=grant),
         name="march",
     )(heat, north, east, vert)
     row = pl.BlockSpec((1, X, Z, L), lambda j: (j, 0, 0, 0))
@@ -474,6 +494,7 @@
         in_specs=[row, pl.BlockSpec((1, Z, L), lambda j: (j, 0, 0))],
         out_specs=(row, row),
         out_shape=(jax.ShapeDtypeStruct((Y, X, Z, L), f32),) * 2,
+        compiler_params=pltpu.CompilerParams(vmem_limit_bytes=8 * 1024 * 1024),
         name="integrate",
     )(end, enter)
 

time: 197 us -> 191 us (0.970); the launches traced: 196 us -> 188 us
  Pallas kernels: 196 us -> 188 us
    pallas_call x1, Pallas kernels: 12.1 us -> 7.6 us  [per_device(): pl.pallas_call(functools.partial(integrate, 1.0 / (X * sizes[1])), grid=(...]
    pallas_call x1, Pallas kernels: 184 us -> 180 us  [per_device(): pl.pallas_call(functools.partial(march, routes, sizes), out_shape=(jax.Sh...]
where the time goes in v3:
time: 191 us; the launch traced here: 188 us
  Pallas kernels  188 us (98%)
    pallas_call x1, Pallas kernels, per_device(): pl.pallas_call(functools.partial(march, routes, sizes), out_shape=(jax.Sh...  180 us
    pallas_call x1, Pallas kernels, per_device(): pl.pallas_call(functools.partial(integrate, 1.0 / (X * sizes[1])), grid=(...  7.6 us

profile of v3, /device:TPU:22, one launch (start us, length us, event | category | flops | bytes accessed | tf_op | source)
XLA Modules:
  0.0 188.4 jit_solution(9443021682499769049)
XLA Ops:
  0.6 180.2 %march.1 = (f32[16,8,96,128]{3,2,1,0:T(8,128)S(1)}, f32[16,96,128]{2,1,0:T(8,128)S(1)}) custom-call(f32[16,8,96,128]{3,2,1,0:T(8,128)} %heat.1, f32[16,8,96,128]{3,2,1,0:T(8,128)} %north.1, f32[16,8,96,128]{3,2,1,0:T(8,128)} %east.1, f32[16,8,96,128]{3,2,1,0:T(8,128)} %vert.1), custom_call_target="tpu_custom_call" | custom-call | tf_op jit(solution)/shard_map/march/pallas_call | solution.py:466
  180.8 7.6 %integrate.1 = (f32[16,8,96,128]{3,2,1,0:T(8,128)}, f32[16,8,96,128]{3,2,1,0:T(8,128)}) custom-call(f32[16,8,96,128]{3,2,1,0:T(8,128)S(1)} %get-tuple-element.4.end_ref, f32[16,96,128]{2,1,0:T(8,128)S(1)} %get-tuple-element.5.enter_ref), custom_call_target="tpu_custom_call" | custom-call | tf_op jit(solution)/shard_map/integrate/pallas_call | solution.py:491
